TPU v7x, 32 devices: a whole 2x2x4 slice. The times are simulated.
32 devices in a mesh: fsdp: 8 (over z, core), tp: 4 (over y, x).
Axes of the slice: x: 2, y: 2, z: 4, core: 2. Of those that a mesh axis runs over, the one named last changes fastest.
Arguments:
- hidden: bfloat16 [3072, 7168], P('fsdp'), may hold values from -72 to 72
- w_query: bfloat16 [7168, 4096], P('fsdp', 'tp'), may hold values from -0.0625 to 0.0625
- w_key: bfloat16 [7168, 1024], P('fsdp', 'tp'), may hold values from -0.0625 to 0.0625
- w_value: bfloat16 [7168, 1024], P('fsdp', 'tp'), may hold values from -0.0625 to 0.0625
- w_out: bfloat16 [4096, 7168], P('tp', 'fsdp'), may hold values from -0.09375 to 0.09375
- exp_query: int32 [56, 32], replicated, may hold values from -1 to 1
- exp_key: int32 [56, 8], replicated, may hold values from -1 to 1
- exp_value: int32 [56, 8], replicated, may hold values from -1 to 1
- exp_out: int32 [32, 56], replicated, may hold values from -1 to 1
- owner: int32 [8], replicated, may hold values from 0 to 7, each once
Outputs:
- attended: bfloat16 [3072, 7168], P('fsdp', 'tp')
Inputs may be any that keep to these rules, and one draw needn't show every extreme that they name: Trainer shard i holds logical slab owner[i]; every slab is held once.
All inputs are finite; a program needn't handle non-finite values.
Results may differ from a plain program's by a relative error of at most 0.038.
Values may be sent and summed in bfloat16 or wider, within the bound.
A program may use at most 128 MiB of HBM per device.

v0:
```python
from functools import partial
import math
import jax
import jax.numpy as jnp
from jax import lax
from jax.sharding import PartitionSpec as P

HQ = 32
HK = 8
HD = 128
neg_large = -1e30


def block_factor(exponents, row_start, row_count, col_start, col_count, block_size):
    repeated = jnp.repeat(exponents, block_size, axis=0)
    picked = lax.dynamic_slice_in_dim(repeated, row_start, row_count, 0)
    repeated = jnp.repeat(picked, block_size, axis=1)
    picked = lax.dynamic_slice_in_dim(repeated, col_start, col_count, 1)
    return jnp.exp2(picked.astype(jnp.float32))


def block_update(state, query_half, pos_half, keys_part, values_part, key_pos, inv_root):
    row_max, row_sum, accum = state
    causal = pos_half[:, None] >= key_pos[None, :]
    scores = (
        jnp.einsum("tgjd,ngd->gjtn", query_half, keys_part, preferred_element_type=jnp.float32)
        * inv_root
    )
    scores = jnp.where(causal, scores, neg_large)
    new_max = jnp.maximum(row_max, jnp.max(scores, axis=3))
    rescale = jnp.exp(row_max - new_max)
    weights = jnp.where(causal, jnp.exp(scores - new_max[..., None]), 0.0)
    row_sum = row_sum * rescale + jnp.sum(weights, axis=3)
    accum = accum * rescale[..., None] + jnp.einsum(
        "gjtn,ngd->gjtd",
        weights.astype(jnp.bfloat16),
        values_part,
        preferred_element_type=jnp.float32,
    )
    return (new_max, row_sum, accum)


def keep_state(state):
    return state


def body(hidden, w_query, w_key, w_value, w_out, exp_query, exp_key, exp_value, exp_out, owner):
    fsdp_index = lax.axis_index("fsdp")
    tp_index = lax.axis_index("tp")
    slab_rows = w_query.shape[0]
    groups = owner.shape[0]
    tokens = hidden.shape[0]
    model_width = hidden.shape[1]
    block_size = model_width // exp_query.shape[0]
    slab_start = owner[fsdp_index] * slab_rows
    query_cols = w_query.shape[1]
    key_cols = w_key.shape[1]

    def scaled_rows(weight, exponents):
        col_count = weight.shape[1]
        factor = block_factor(
            exponents, slab_start, slab_rows, tp_index * col_count, col_count, block_size
        )
        return (weight.astype(jnp.float32) * factor).astype(jnp.bfloat16)

    query_local = scaled_rows(w_query, exp_query)
    key_local = scaled_rows(w_key, exp_key)
    value_local = scaled_rows(w_value, exp_value)
    out_rows = w_out.shape[0]
    out_factor = block_factor(
        exp_out, tp_index * out_rows, out_rows, slab_start, slab_rows, block_size
    )
    out_local = (w_out.astype(jnp.float32) * out_factor).astype(jnp.bfloat16)
    arranged = jnp.take(hidden.reshape(tokens, groups, slab_rows), owner, axis=1).reshape(
        tokens, model_width
    )
    pieces = (
        lax.all_gather(query_local, "fsdp", axis=0, tiled=True),
        lax.all_gather(key_local, "fsdp", axis=0, tiled=True),
        lax.all_gather(value_local, "fsdp", axis=0, tiled=True),
    )
    query_sum, key_sum, value_sum = tuple(
        (jnp.dot(arranged, weight, preferred_element_type=jnp.float32) for weight in pieces)
    )
    query = query_sum.astype(jnp.bfloat16)
    key_here = key_sum.astype(jnp.bfloat16)
    value_here = value_sum.astype(jnp.bfloat16)
    half_rows = tokens // 2
    local_pos = fsdp_index * tokens + jnp.arange(tokens, dtype=jnp.int32)
    group_size = HQ // HK
    kv_heads = key_cols // HD
    query_halves = query.reshape(2, half_rows, kv_heads, group_size, HD)
    pos_halves = local_pos.reshape(2, half_rows)
    pos_top = jnp.max(pos_halves, axis=1)
    inv_root = 1.0 / math.sqrt(HD)
    one_state = (
        jnp.full((kv_heads, group_size, half_rows), neg_large, jnp.float32),
        jnp.zeros((kv_heads, group_size, half_rows), jnp.float32),
        jnp.zeros((kv_heads, group_size, half_rows, HD), jnp.float32),
    )
    offset = jnp.int32(0)
    key_piece = lax.all_gather(key_here, "fsdp", axis=0, tiled=True)
    value_piece = lax.all_gather(value_here, "fsdp", axis=0, tiled=True)
    states = list((one_state, one_state))
    piece_rows = key_piece.shape[0]
    for block_low in range(0, piece_rows, 1024):
        block_high = min(block_low + 1024, piece_rows)
        width_here = block_high - block_low
        keys_part = key_piece[block_low:block_high].reshape(width_here, kv_heads, HD)
        values_part = value_piece[block_low:block_high].reshape(width_here, kv_heads, HD)
        key_pos = offset + block_low + jnp.arange(width_here, dtype=jnp.int32)
        for attend_which in range(2):
            update = partial(
                block_update,
                query_half=query_halves[attend_which],
                pos_half=pos_halves[attend_which],
                keys_part=keys_part,
                values_part=values_part,
                key_pos=key_pos,
                inv_root=inv_root,
            )
            states[attend_which] = lax.cond(
                offset + block_low <= pos_top[attend_which],
                update,
                keep_state,
                states[attend_which],
            )
    final_states = tuple(states)
    context_parts = []
    for which in range(2):
        row_max, row_sum, accum = final_states[which]
        part_context = (accum / row_sum[..., None]).astype(jnp.bfloat16)
        context_parts.append(part_context.transpose(2, 0, 1, 3).reshape(half_rows, query_cols))
    context = jnp.concatenate(context_parts, axis=0)
    column_terms = jnp.dot(
        context,
        lax.all_gather(out_local, "fsdp", axis=1, tiled=True),
        preferred_element_type=jnp.float32,
    )
    slab_ids = jnp.arange(groups, dtype=jnp.int32)
    inverse = jnp.sum(
        slab_ids[:, None] * (owner[:, None] == slab_ids[None, :]).astype(jnp.int32), axis=0
    )
    ordered = jnp.take(column_terms.reshape(tokens, groups, slab_rows), inverse, axis=1).reshape(
        tokens, model_width
    )
    result = lax.psum_scatter(ordered.astype(jnp.bfloat16), "tp", scatter_dimension=1, tiled=True)
    return result


def solution(mesh):
    placed = (
        P("fsdp", None),
        P("fsdp", "tp"),
        P("fsdp", "tp"),
        P("fsdp", "tp"),
        P("tp", "fsdp"),
        P(),
        P(),
        P(),
        P(),
        P(),
    )
    return jax.shard_map(
        body, mesh=mesh, in_specs=placed, out_specs=P("fsdp", "tp"), check_vma=False
    )
```

profile of v0, /device:TPU:0, one launch (start us, length us, event | category | flops | bytes accessed | tf_op | source)
XLA Modules:
  0.0 532.7 jit_solution(14240318342266903279)
XLA Ops:
  11.6 2.7 copy.224
  19.4 8.3 %copy.85 = bf16[384,7168]{0,1:T(8,128)(2,1)} copy(bf16[384,7168]{1,0:T(8,128)(2,1)} %param.22) | data formatting | bytes 11010048 | tf_op args[0]
  27.7 8.1 %copy.86 = bf16[384,8,896]{2,0,1:T(8,128)(2,1)} copy(bf16[384,8,896]{0,2,1:T(8,128)(2,1)} %bitcast.184) | data formatting | bytes 11010048 | tf_op jit(solution)/shard_map/reshape | solution.py:74
  35.8 6.3 %gather_fusion = bf16[8,384,896]{2,1,0:T(8,128)(2,1)} fusion(bf16[384,8,896]{2,0,1:T(8,128)(2,1)} %copy.86, s32[1024]{0:T(1024)S(1)} %pad_clamp_fusion.1), kind=kCustom, calls=%fused_computation | custom fusion | bytes 11010080 | tf_op jit(solution)/shard_map/jit(_take)/gather | solution.py:74
  42.1 8.4 %copy.87 = bf16[384,8,896]{0,2,1:T(8,128)(2,1)} copy(bf16[384,8,896]{2,0,1:T(8,128)(2,1)} %bitcast.181) | data formatting | bytes 11010048 | tf_op jit(solution)/shard_map/jit(_take)/gather | solution.py:74
  50.7 7.3 %bitcast_select_fusion.7 = bf16[384,7168]{0,1:T(8,128)(2,1)} fusion(bf16[384,8,896]{0,2,1:T(8,128)(2,1)} %copy.87, pred[7168]{0:T(1024)(128)(4,1)S(1)} %broadcast_in_dim.175), kind=kLoop, calls=%fused_computation.117 | loop fusion | flops 2752512 | bytes 11017216 | tf_op jit(solution)/shard_map/jit(_take)/select_n | solution.py:74
  58.1 3.8 all-gather.7.cloned.1.call-done
  61.8 6.0 %convolution_convert_fusion.2 = bf16[384,256]{1,0:T(8,128)(2,1)} fusion(bf16[384,7168]{0,1:T(8,128)(2,1)} %bitcast_select_fusion.7, bf16[7168,256]{1,0:T(8,128)(2,1)} %all-gather.7.cloned.1.call-done), kind=kOutput, calls=%fused_computation.124 | convolution fusion | flops 1409384448 | bytes 9371648 | tf_op jit(solution)/shard_map/dot_general | solution.py:83
  67.9 37.0 %all-gather.13.cloned.1.call-done = bf16[7168,256]{1,0:T(8,128)(2,1)} async-done(((bf16[896,256]{1,0:T(8,128)(2,1)}), bf16[7168,256]{1,0:T(8,128)(2,1)}) %all-gather.13.cloned.1.call-update) | async-done | bytes 3670032 | tf_op jit(solution)/shard_map/all_gather | solution.py:80
  104.8 6.0 %convolution_convert_fusion.1 = bf16[384,256]{1,0:T(8,128)(2,1)} fusion(bf16[384,7168]{0,1:T(8,128)(2,1)} %bitcast_select_fusion.7, bf16[7168,256]{1,0:T(8,128)(2,1)} %all-gather.13.cloned.1.call-done), kind=kOutput, calls=%fused_computation.123 | convolution fusion | flops 1409384448 | bytes 9371648 | tf_op jit(solution)/shard_map/dot_general | solution.py:83
  111.3 6.4 %broadcast_in_dim.182 = s32[896,32,128]{2,1,0:T(8,128)} broadcast(s32[896,32]{1,0:T(8,128)S(1)} %constant_dynamic-slice_fusion.2), dimensions={0,1} | broadcast | bytes 14794752 | tf_op jit(solution)/shard_map/broadcast_in_dim | solution.py:17
  117.7 25.4 %copy.221 = s32[112,8,32,128]{3,1,2,0:T(8,128)} copy(s32[112,8,32,128]{3,2,1,0:T(8,128)} %bitcast.178) | data formatting | bytes 29360128
  143.1 4.1 multiply_convert_fusion.1
  147.5 8.0 %broadcast_in_dim.186 = s32[1024,56,128]{2,1,0:T(8,128)S(1)} broadcast(s32[1024,56]{1,0:T(8,128)S(1)} %constant_dynamic-slice_fusion), dimensions={0,1} | broadcast | bytes 29589504 | tf_op jit(solution)/shard_map/broadcast_in_dim | solution.py:17
  155.6 13.7 %copy.220 = s32[128,8,56,128]{3,1,2,0:T(8,128)} copy(s32[128,8,56,128]{3,2,1,0:T(8,128)S(1)} %bitcast.177) | data formatting | bytes 58720256
  169.3 4.2 multiply_convert_fusion
  186.3 104.8 %all-gather.11.cloned.1.call-done = bf16[7168,1024]{1,0:T(8,128)(2,1)} async-done(((bf16[896,1024]{1,0:T(8,128)(2,1)}), bf16[7168,1024]{1,0:T(8,128)(2,1)}) %all-gather.11.cloned.1.call-update) | async-done | bytes 14680080 | tf_op jit(solution)/shard_map/all_gather | solution.py:78
  291.1 10.7 %convolution_convert_fusion = bf16[384,1024]{1,0:T(8,128)(2,1)S(1)} fusion(bf16[384,7168]{0,1:T(8,128)(2,1)} %bitcast_select_fusion.7, bf16[7168,1024]{1,0:T(8,128)(2,1)} %all-gather.11.cloned.1.call-done), kind=kOutput, calls=%fused_computation.122 | convolution fusion | flops 5637537792 | bytes 20971520 | tf_op jit(solution)/shard_map/dot_general | solution.py:83
  302.2 9.8 %conditional.9 = (f32[2,4,192]{2,1,0:T(4,128)}, f32[2,4,192]{2,1,0:T(4,128)S(1)}, f32[2,4,192,128]{3,2,1,0:T(8,128)S(1)}) conditional(s32[]{:T(128)} %bitcast.38, () %tuple.52, (s32[1,192]{1,0:T(1,128)S(1)}, s32[1024]{0:T(1024)S(1)}, bf16[1024,2,128]{2,1,0:T(2,128)(2,1)}, bf16[192,2,4,128]{3,2,1,0:T(4,128)(2,1)S(1)}, ...), branch_computations={%region_14.15_spmd, %region_15.18_spmd} | conditional | flops 826152960 | bytes 24058676 | solution.py:122
  305.5 2.8 fusion.51
  309.0 2.7 fusion.55
  313.9 15.2 %conditional.6 = (f32[2,4,192]{2,1,0:T(4,128)}, f32[2,4,192]{2,1,0:T(4,128)S(1)}, f32[2,4,192,128]{3,2,1,0:T(8,128)S(1)}) conditional(s32[]{:T(128)} %bitcast.26, () %tuple.47, (s32[1,192]{1,0:T(1,128)}, s32[1024]{0:T(1024)S(1)}, bf16[1024,2,128]{2,1,0:T(2,128)(2,1)}, bf16[192,2,4,128]{3,2,1,0:T(4,128)(2,1)}, bf16[1024,2,128]{2,1,0:T(2,128)(2,1)}) %tuple.147), branch_computations={%region_2.3_spmd, %region_3.6_spmd} | conditional | flops 826152960 | bytes 24058676 | solution.py:122
  319.7 2.6 fusion
  322.9 2.8 fusion.2
  326.4 2.7 fusion.6
  330.8 93.8 %all-gather.17.cloned.1.call-done = bf16[1024,7168]{1,0:T(8,128)(2,1)} async-done(((bf16[1024,896]{1,0:T(8,128)(2,1)}), bf16[1024,7168]{1,0:T(8,128)(2,1)}) %all-gather.17.cloned.1.call-update) | async-done | bytes 14680080 | tf_op jit(solution)/shard_map/all_gather | solution.py:137
  424.6 11.6 %fusion.99 = bf16[384,7168]{1,0:T(8,128)(2,1)S(1)} fusion(bf16[1024,7168]{1,0:T(8,128)(2,1)} %all-gather.17.cloned.1.call-done, bf16[192,1024]{1,0:T(8,128)(2,1)S(1)} %reshape.169, bf16[192,1024]{1,0:T(8,128)(2,1)S(1)} %reshape.168), kind=kOutput, calls=%fused_computation.127 | convolution fusion | flops 5638717440 | bytes 20971520 | tf_op jit(solution)/shard_map/dot_general | solution.py:135
  436.2 3.2 copy.222
  439.5 6.3 %gather_fusion.1 = bf16[8,384,896]{2,1,0:T(8,128)(2,1)} fusion(bf16[384,8,896]{2,0,1:T(8,128)(2,1)} %bitcast.182, s32[1024]{0:T(1024)} %pad_clamp_fusion), kind=kCustom, calls=%fused_computation.1 | custom fusion | bytes 11010080 | tf_op jit(solution)/shard_map/jit(_take)/gather | solution.py:144
  445.7 8.3 %copy.112 = bf16[384,8,896]{0,2,1:T(8,128)(2,1)} copy(bf16[384,8,896]{2,0,1:T(8,128)(2,1)} %bitcast.183) | data formatting | bytes 11010048 | tf_op jit(solution)/shard_map/jit(_take)/gather | solution.py:144
  454.0 7.3 %fusion.98 = bf16[384,7168]{0,1:T(8,128)(2,1)} fusion(bf16[384,8,896]{0,2,1:T(8,128)(2,1)} %copy.112, pred[7168]{0:T(1024)(128)(4,1)S(1)} %copy-done.14), kind=kLoop, calls=%fused_computation.116 | loop fusion | flops 2752512 | bytes 11017216 | tf_op jit(solution)/shard_map/convert_element_type | solution.py:147
  461.4 61.8 %reduce-scatter.2.cloned.1.call-done = bf16[384,1792]{0,1:T(8,128)(2,1)} async-done(((bf16[384,7168]{0,1:T(8,128)(2,1)}), bf16[384,1792]{0,1:T(8,128)(2,1)}) %reduce-scatter.2.cloned.1.call-update) | async-done | bytes 1376272 | tf_op jit(solution)/shard_map/reduce_scatter | solution.py:147
  (111 shorter events, 31.9 us)
Async XLA Ops:
  6.5 140.8 %copy-start = (s32[32,56]{1,0:T(8,128)S(1)}, s32[32,56]{1,0:T(8,128)}, u32[]{:S(2)}) copy-start(s32[32,56]{1,0:T(8,128)} %param.30) | copy-start | bytes 21508
  6.5 55.3 %all-gather.7.cloned.1.call-start = ((), (), s32[]{:S(2)}) async-start(), calls=%async_computation.1 | async-start | bytes 4128768 | tf_op jit(solution)/shard_map/all_gather | solution.py:79
  10.5 3.8 copy-start.8
  16.4 2.0 copy-start.9
  16.4 88.4 %all-gather.13.cloned.1.call-start = ((), (), s32[]{:S(2)}) async-start(), calls=%async_computation.4 | async-start | bytes 4128768 | tf_op jit(solution)/shard_map/all_gather | solution.py:80
  19.4 160.9 %all-gather.9.cloned.1.call-start = ((), (), s32[]{:S(2)}) async-start(), calls=%async_computation.2 | async-start | bytes 1769472 | tf_op jit(solution)/shard_map/all_gather | solution.py:102
  27.7 8.1 %copy-start.16 = (s32[8]{0:T(128)S(1)}, s32[8]{0:T(128)}, u32[]{:S(2)}) copy-start(s32[8]{0:T(128)} %param.31) | copy-start | bytes 100
  67.8 43.1 %copy-start.15 = (s32[56,32]{0,1:T(8,128)S(1)}, s32[56,32]{0,1:T(8,128)}, u32[]{:S(2)}) copy-start(s32[56,32]{0,1:T(8,128)} %param.27) | copy-start | bytes 21508
  67.8 114.8 %all-gather.15.cloned.1.call-start = ((), (), s32[]{:S(2)}) async-start(), calls=%async_computation.5 | async-start | bytes 1769472 | tf_op jit(solution)/shard_map/all_gather | solution.py:103
  110.9 180.2 %all-gather.11.cloned.1.call-start = ((), (), s32[]{:S(2)}) async-start(), calls=%async_computation.3 | async-start | bytes 16515072 | tf_op jit(solution)/shard_map/all_gather | solution.py:78
  117.7 25.4 %copy-start.2 = (bf16[896,1024]{1,0:T(8,128)(2,1)S(1)}, bf16[896,1024]{1,0:T(8,128)(2,1)}, u32[]{:S(2)}) copy-start(bf16[896,1024]{1,0:T(8,128)(2,1)} %param.23) | copy-start | bytes 5505028
  147.3 277.4 %all-gather.17.cloned.1.call-start = ((), (), s32[]{:S(2)}) async-start(), calls=%async_computation.6 | async-start | bytes 16515072 | tf_op jit(solution)/shard_map/all_gather | solution.py:137
  155.6 13.7 %copy-start.3 = (bf16[1024,896]{1,0:T(8,128)(2,1)S(1)}, bf16[1024,896]{1,0:T(8,128)(2,1)}, u32[]{:S(2)}) copy-start(bf16[1024,896]{1,0:T(8,128)(2,1)} %param.26) | copy-start | bytes 5505028
  173.5 349.7 %reduce-scatter.2.cloned.1.call-start = ((), (), s32[]{:S(2)}) async-start(), calls=%async_computation.7 | async-start | bytes 6881280 | tf_op jit(solution)/shard_map/reduce_scatter | solution.py:147
  179.0 132.9 %copy-start.12 = (s32[1024]{0:T(1024)}, s32[1024]{0:T(1024)S(1)}, u32[]{:S(2)}) copy-start(s32[1024]{0:T(1024)S(1)} %iota_add_fusion.1) | copy-start | bytes 12292
  179.0 132.9 %copy-start.10 = (s32[1024]{0:T(1024)}, s32[1024]{0:T(1024)S(1)}, u32[]{:S(2)}) copy-start(s32[1024]{0:T(1024)S(1)} %iota_add_fusion) | copy-start | bytes 12292
  302.4 6.6 %copy-start.6 = (bf16[1024,2,128]{2,1,0:T(2,128)(2,1)S(1)}, bf16[1024,2,128]{2,1,0:T(2,128)(2,1)}, u32[]{:S(2)}) copy-start(bf16[1024,2,128]{2,1,0:T(2,128)(2,1)} %get-tuple-element.334) | copy-start | bytes 1572868 | tf_op jit(solution)/shard_map/cond
  313.9 15.2 %copy-start.4 = (bf16[1024,2,128]{2,1,0:T(2,128)(2,1)S(1)}, bf16[1024,2,128]{2,1,0:T(2,128)(2,1)}, u32[]{:S(2)}) copy-start(bf16[1024,2,128]{2,1,0:T(2,128)(2,1)} %reshape.165) | copy-start | bytes 1572868
  313.9 15.2 %copy-start.13 = (s32[1024]{0:T(1024)S(1)}, s32[1024]{0:T(1024)}, u32[]{:S(2)}) copy-start(s32[1024]{0:T(1024)} %copy-done.12) | copy-start | bytes 12292
  319.7 6.7 %copy-start.7 = (bf16[1024,2,128]{2,1,0:T(2,128)(2,1)S(1)}, bf16[1024,2,128]{2,1,0:T(2,128)(2,1)}, u32[]{:S(2)}) copy-start(bf16[1024,2,128]{2,1,0:T(2,128)(2,1)} %get-tuple-element.313) | copy-start | bytes 1572868 | tf_op jit(solution)/shard_map/cond
  329.1 0.7 copy-start.11
  445.7 8.3 %copy-start.14 = (pred[7168]{0:T(1024)(128)(4,1)S(1)}, pred[7168]{0:T(1024)(128)(4,1)}, u32[]{:S(2)}) copy-start(pred[7168]{0:T(1024)(128)(4,1)} %broadcast_in_dim.172) | copy-start | bytes 21508
  454.0 71.7 %copy-start.1 = (s32[32,56]{1,0:T(8,128)S(1)}, s32[32,56]{1,0:T(8,128)}, u32[]{:S(2)}) copy-start(s32[32,56]{1,0:T(8,128)} %param.30) | copy-start | bytes 21508
Sparse Core Ops, SparseCore 0:
  16.5 45.2 all-gather.6
  63.5 41.3 all-gather.12
  106.5 24.0 all-gather.8
  132.1 24.3 all-gather.14
  158.0 133.0 all-gather.10
  292.5 132.0 all-gather.16
  461.5 61.6 reduce-scatter.1
where the time goes:
time: 543 us; the launch traced here: 533 us
  waiting for transfers between devices  301 us (55%)
  local copies, waits for them, and re-layouts  126 us (23%)
  matrix products  44.8 us (8%)
  other arithmetic  36.7 us (7%)
  between operations  18.7 us (3%)
    all_gather x1, waiting for transfers between devices, body(): lax.all_gather(query_local, 'fsdp', axis=0, tiled=True)  105 us
    all_gather x1, waiting for transfers between devices, body(): lax.all_gather(out_local, 'fsdp', axis=1, tiled=True)  93.8 us
    reduce_scatter x1, waiting for transfers between devices, body(): lax.psum_scatter(ordered.astype(jnp.bfloat16), 'tp', scatter_dimension=1,...  61.8 us
    unnamed x36, local copies, waits for them, and re-layouts  53.3 us
    all_gather x1, waiting for transfers between devices, body(): lax.all_gather(value_local, 'fsdp', axis=0, tiled=True)  37 us
    dot_general x3, matrix products, body(): jnp.dot(arranged, weight, preferred_element_type=jnp.float32)  22.7 us
    broadcast_in_dim x4, local copies, waits for them, and re-layouts, block_factor(): repeated = jnp.repeat(picked, block_size, axis=1)  16.5 us
    gather x2, local copies, waits for them, and re-layouts, body(): jnp.take(hidden.reshape(tokens, groups, slab_rows), owner, axis=1)  14.7 us
  transfers between devices with their start and end apart: 7, of which 5 were waited for; matrix products, arithmetic and copies ran while one was open for 30% of the time, Pallas kernels for 0%

commit v1 on v0

--- a/solution.py
+++ b/solution.py
@@ -134,7 +134,9 @@
     context = jnp.concatenate(context_parts, axis=0)
     column_terms = jnp.dot(
         context,
-        lax.all_gather(out_local, "fsdp", axis=1, tiled=True),
+        jnp.concatenate(
+            lax.all_to_all(jnp.stack([out_local] * lax.axis_size("fsdp")), "fsdp", 0, 0), axis=1
+        ),
         preferred_element_type=jnp.float32,
     )
     slab_ids = jnp.arange(groups, dtype=jnp.int32)

time: 543 us -> 728 us (1.34)
  waiting for transfers between devices: 301 us -> 468 us
  matrix products: 44.8 us -> 54.3 us
    all_to_all x0 -> x1, waiting for transfers between devices: none -> 175 us  [body(): lax.all_to_all(jnp.stack([out_local] * lax.axis_size('fsdp')), 'fsdp', 0, 0)]
    all_gather x1 -> x0, waiting for transfers between devices: 93.8 us -> none  [body(): lax.all_gather(out_local, 'fsdp', axis=1, tiled=True)]
    all_gather x1, waiting for transfers between devices: 105 us -> 190 us  [body(): lax.all_gather(query_local, 'fsdp', axis=0, tiled=True)]
    dot_general x1, matrix products: 11.6 us -> 21.1 us  [body(): jnp.dot(context, jnp.concatenate(lax.all_to_all(jnp.stack([out_local] * l...]
  transfers between devices with their start and end apart: 7 -> 7, of which waited for: 5 -> 5; matrix products, arithmetic and copies ran while one was open for 30% -> 23% of each run, Pallas kernels for 0% -> 0%
where the time goes in v1:
time: 728 us; the launch traced here: 718 us
  waiting for transfers between devices  468 us (64%)
  local copies, waits for them, and re-layouts  131 us (18%)
  matrix products  54.3 us (7%)
  other arithmetic  35.4 us (5%)
  between operations  18.3 us (3%)
    all_gather x1, waiting for transfers between devices, body(): lax.all_gather(query_local, 'fsdp', axis=0, tiled=True)  190 us
    all_to_all x1, waiting for transfers between devices, body(): lax.all_to_all(jnp.stack([out_local] * lax.axis_size('fsdp')), 'fsdp', 0, 0)  175 us
    reduce_scatter x1, waiting for transfers between devices, body(): lax.psum_scatter(ordered.astype(jnp.bfloat16), 'tp', scatter_dimension=1,...  61.8 us
    unnamed x36, local copies, waits for them, and re-layouts  53.2 us
    all_gather x1, waiting for transfers between devices, body(): lax.all_gather(value_local, 'fsdp', axis=0, tiled=True)  37 us
    dot_general x3, matrix products, body(): jnp.dot(arranged, weight, preferred_element_type=jnp.float32)  22.7 us
    dot_general x1, matrix products, body(): jnp.dot(context, jnp.concatenate(lax.all_to_all(jnp.stack([out_local] * l...  21.1 us
    broadcast_in_dim x4, local copies, waits for them, and re-layouts, block_factor(): repeated = jnp.repeat(picked, block_size, axis=1)  16.5 us
  transfers between devices with their start and end apart: 7, of which 5 were waited for; matrix products, arithmetic and copies ran while one was open for 23% of the time, Pallas kernels for 0%

profile of v1, /device:TPU:0, one launch (start us, length us, event | category | flops | bytes accessed | tf_op | source)
XLA Modules:
  0.0 717.9 jit_solution(16967294579019868197)
XLA Ops:
  11.6 2.7 copy.226
  19.4 8.3 %copy.90 = bf16[384,7168]{0,1:T(8,128)(2,1)} copy(bf16[384,7168]{1,0:T(8,128)(2,1)} %param.22) | data formatting | bytes 11010048 | tf_op args[0]
  27.7 8.0 %copy.91 = bf16[384,8,896]{2,0,1:T(8,128)(2,1)} copy(bf16[384,8,896]{0,2,1:T(8,128)(2,1)} %bitcast.190) | data formatting | bytes 11010048 | tf_op jit(solution)/shard_map/reshape | solution.py:74
  35.7 6.3 gather_fusion
  42.0 8.3 %copy.92 = bf16[384,8,896]{0,2,1:T(8,128)(2,1)} copy(bf16[384,8,896]{2,0,1:T(8,128)(2,1)} %bitcast.188) | data formatting | bytes 11010048 | tf_op jit(solution)/shard_map/jit(_take)/gather | solution.py:74
  50.6 7.3 %bitcast_select_fusion.7 = bf16[384,7168]{0,1:T(8,128)(2,1)} fusion(bf16[384,8,896]{0,2,1:T(8,128)(2,1)} %copy.92, pred[7168]{0:T(1024)(128)(4,1)S(1)} %broadcast_in_dim.175), kind=kLoop, calls=%fused_computation.118 | loop fusion | flops 2752512 | bytes 11017216 | tf_op jit(solution)/shard_map/jit(_take)/select_n | solution.py:74
  57.8 4.0 all-gather.6.cloned.1.call-done
  61.8 6.0 convolution_convert_fusion.2
  67.9 37.0 %all-gather.12.cloned.1.call-done = bf16[7168,256]{1,0:T(8,128)(2,1)} async-done(((bf16[896,256]{1,0:T(8,128)(2,1)}), bf16[7168,256]{1,0:T(8,128)(2,1)}) %all-gather.12.cloned.1.call-update) | async-done | bytes 3670032 | tf_op jit(solution)/shard_map/all_gather | solution.py:80
  104.8 6.0 convolution_convert_fusion.1
  111.3 6.4 broadcast_in_dim.182
  117.7 25.4 %copy.224 = s32[112,8,32,128]{3,1,2,0:T(8,128)} copy(s32[112,8,32,128]{3,2,1,0:T(8,128)} %bitcast.185) | data formatting | bytes 29360128
  143.1 4.1 multiply_convert_fusion.1
  147.5 8.0 %broadcast_in_dim.186 = s32[1024,56,128]{2,1,0:T(8,128)S(1)} broadcast(s32[1024,56]{1,0:T(8,128)S(1)} %constant_dynamic-slice_fusion), dimensions={0,1} | broadcast | bytes 29589504 | tf_op jit(solution)/shard_map/broadcast_in_dim | solution.py:17
  155.5 13.7 %copy.223 = s32[128,8,56,128]{3,1,2,0:T(8,128)} copy(s32[128,8,56,128]{3,2,1,0:T(8,128)S(1)} %bitcast.184) | data formatting | bytes 58720256
  169.2 2.9 multiply_convert_fusion
  174.7 6.5 stack.2
  181.2 5.6 all-to-all-start
  199.2 189.8 %all-gather.10.cloned.1.call-done = bf16[7168,1024]{1,0:T(8,128)(2,1)} async-done(((bf16[896,1024]{1,0:T(8,128)(2,1)}), bf16[7168,1024]{1,0:T(8,128)(2,1)}) %all-gather.10.cloned.1.call-update) | async-done | bytes 14680080 | tf_op jit(solution)/shard_map/all_gather | solution.py:78
  388.9 10.7 %convolution_convert_fusion = bf16[384,1024]{1,0:T(8,128)(2,1)S(1)} fusion(bf16[384,7168]{0,1:T(8,128)(2,1)} %bitcast_select_fusion.7, bf16[7168,1024]{1,0:T(8,128)(2,1)} %all-gather.10.cloned.1.call-done), kind=kOutput, calls=%fused_computation.123 | convolution fusion | flops 5637537792 | bytes 20971520 | tf_op jit(solution)/shard_map/dot_general | solution.py:83
  400.0 9.7 %conditional.9 = (f32[2,4,192]{2,1,0:T(4,128)}, f32[2,4,192]{2,1,0:T(4,128)S(1)}, f32[2,4,192,128]{3,2,1,0:T(8,128)S(1)}) conditional(s32[]{:T(128)} %bitcast.38, () %tuple.52, (s32[1,192]{1,0:T(1,128)S(1)}, s32[1024]{0:T(1024)S(1)}, bf16[1024,2,128]{2,1,0:T(2,128)(2,1)}, bf16[192,2,4,128]{3,2,1,0:T(4,128)(2,1)S(1)}, ...), branch_computations={%region_14.15_spmd, %region_15.18_spmd} | conditional | flops 826152960 | bytes 24058676 | solution.py:122
  403.3 2.8 fusion.51
  406.8 2.7 fusion.55
  411.7 15.1 %conditional.6 = (f32[2,4,192]{2,1,0:T(4,128)}, f32[2,4,192]{2,1,0:T(4,128)S(1)}, f32[2,4,192,128]{3,2,1,0:T(8,128)S(1)}) conditional(s32[]{:T(128)} %bitcast.26, () %tuple.47, (s32[1,192]{1,0:T(1,128)}, s32[1024]{0:T(1024)S(1)}, bf16[1024,2,128]{2,1,0:T(2,128)(2,1)}, bf16[192,2,4,128]{3,2,1,0:T(4,128)(2,1)}, bf16[1024,2,128]{2,1,0:T(2,128)(2,1)}) %tuple.145), branch_computations={%region_2.3_spmd, %region_3.6_spmd} | conditional | flops 826152960 | bytes 24058676 | solution.py:122
  420.7 2.8 fusion.2
  424.2 2.7 fusion.6
  428.6 175.0 %all-to-all-done = bf16[8,1024,896]{1,2,0:T(8,128)(2,1)} async-done(((bf16[8,1024,896]{1,2,0:T(8,128)(2,1)}), bf16[8,1024,896]{1,2,0:T(8,128)(2,1)}, u32[]{:S(2)}, u32[]{:S(2)}) %all-to-all-start) | async-done | bytes 14680096 | tf_op jit(solution)/shard_map/all_to_all | solution.py:138
  603.6 21.1 %fusion.98 = bf16[384,8,896]{2,0,1:T(8,128)(2,1)} fusion(bf16[8,1024,896]{1,2,0:T(8,128)(2,1)} %all-to-all-done, bf16[192,1024]{1,0:T(8,128)(2,1)S(1)} %reshape.176, bf16[192,1024]{1,0:T(8,128)(2,1)S(1)} %reshape.175), kind=kOutput, calls=%fused_computation.114 | convolution fusion | flops 5638717440 | bytes 20971520 | tf_op jit(solution)/shard_map/dot_general | solution.py:135
  624.7 6.3 gather_fusion.1
  631.0 8.3 %copy.117 = bf16[384,8,896]{0,2,1:T(8,128)(2,1)} copy(bf16[384,8,896]{2,0,1:T(8,128)(2,1)} %bitcast.189) | data formatting | bytes 11010048 | tf_op jit(solution)/shard_map/jit(_take)/gather | solution.py:146
  639.3 7.3 %fusion.100 = bf16[384,7168]{0,1:T(8,128)(2,1)} fusion(bf16[384,8,896]{0,2,1:T(8,128)(2,1)} %copy.117, pred[7168]{0:T(1024)(128)(4,1)S(1)} %copy-done.14), kind=kLoop, calls=%fused_computation.117 | loop fusion | flops 2752512 | bytes 11017216 | tf_op jit(solution)/shard_map/convert_element_type | solution.py:149
  646.6 61.8 %reduce-scatter.2.cloned.1.call-done = bf16[384,1792]{0,1:T(8,128)(2,1)} async-done(((bf16[384,7168]{0,1:T(8,128)(2,1)}), bf16[384,1792]{0,1:T(8,128)(2,1)}) %reduce-scatter.2.cloned.1.call-update) | async-done | bytes 1376272 | tf_op jit(solution)/shard_map/reduce_scatter | solution.py:149
  (111 shorter events, 36.9 us)
Async XLA Ops:
  6.5 140.7 %copy-start = (s32[32,56]{1,0:T(8,128)S(1)}, s32[32,56]{1,0:T(8,128)}, u32[]{:S(2)}) copy-start(s32[32,56]{1,0:T(8,128)} %param.30) | copy-start | bytes 21508
  6.5 55.3 %all-gather.6.cloned.1.call-start = ((), (), s32[]{:S(2)}) async-start(), calls=%async_computation.2 | async-start | bytes 4128768 | tf_op jit(solution)/shard_map/all_gather | solution.py:79
  10.5 3.8 copy-start.8
  16.4 2.0 copy-start.9
  16.4 88.4 %all-gather.12.cloned.1.call-start = ((), (), s32[]{:S(2)}) async-start(), calls=%async_computation.5 | async-start | bytes 4128768 | tf_op jit(solution)/shard_map/all_gather | solution.py:80
  19.3 173.7 %all-gather.8.cloned.1.call-start = ((), (), s32[]{:S(2)}) async-start(), calls=%async_computation.3 | async-start | bytes 1769472 | tf_op jit(solution)/shard_map/all_gather | solution.py:102
  27.7 8.0 %copy-start.16 = (s32[8]{0:T(128)S(1)}, s32[8]{0:T(128)}, u32[]{:S(2)}) copy-start(s32[8]{0:T(128)} %param.31) | copy-start | bytes 100
  67.8 43.1 %copy-start.15 = (s32[56,32]{0,1:T(8,128)S(1)}, s32[56,32]{0,1:T(8,128)}, u32[]{:S(2)}) copy-start(s32[56,32]{0,1:T(8,128)} %param.27) | copy-start | bytes 21508
  67.8 127.6 %all-gather.14.cloned.1.call-start = ((), (), s32[]{:S(2)}) async-start(), calls=%async_computation.6 | async-start | bytes 1769472 | tf_op jit(solution)/shard_map/all_gather | solution.py:103
  110.8 278.1 %all-gather.10.cloned.1.call-start = ((), (), s32[]{:S(2)}) async-start(), calls=%async_computation.4 | async-start | bytes 16515072 | tf_op jit(solution)/shard_map/all_gather | solution.py:78
  117.7 25.4 %copy-start.2 = (bf16[896,1024]{1,0:T(8,128)(2,1)S(1)}, bf16[896,1024]{1,0:T(8,128)(2,1)}, u32[]{:S(2)}) copy-start(bf16[896,1024]{1,0:T(8,128)(2,1)} %param.23) | copy-start | bytes 5505028
  155.5 13.7 %copy-start.3 = (bf16[1024,896]{1,0:T(8,128)(2,1)S(1)}, bf16[1024,896]{1,0:T(8,128)(2,1)}, u32[]{:S(2)}) copy-start(bf16[1024,896]{1,0:T(8,128)(2,1)} %param.26) | copy-start | bytes 5505028
  181.2 422.4 %all-to-all-start = ((bf16[8,1024,896]{1,2,0:T(8,128)(2,1)}), bf16[8,1024,896]{1,2,0:T(8,128)(2,1)}, u32[]{:S(2)}, u32[]{:S(2)}) async-start(bf16[8,1024,896]{1,2,0:T(8,128)(2,1)} %stack.2), calls=%async_computation | async-start | bytes 29360128 | tf_op jit(solution)/shard_map/all_to_all | solution.py:138
  186.8 521.6 %reduce-scatter.2.cloned.1.call-start = ((), (), s32[]{:S(2)}) async-start(), calls=%async_computation.7 | async-start | bytes 6881280 | tf_op jit(solution)/shard_map/reduce_scatter | solution.py:149
  191.9 217.9 %copy-start.12 = (s32[1024]{0:T(1024)}, s32[1024]{0:T(1024)S(1)}, u32[]{:S(2)}) copy-start(s32[1024]{0:T(1024)S(1)} %iota_add_fusion.1) | copy-start | bytes 12292
  191.9 217.9 %copy-start.10 = (s32[1024]{0:T(1024)}, s32[1024]{0:T(1024)S(1)}, u32[]{:S(2)}) copy-start(s32[1024]{0:T(1024)S(1)} %iota_add_fusion) | copy-start | bytes 12292
  400.2 6.6 copy-start.6
  411.7 15.1 %copy-start.4 = (bf16[1024,2,128]{2,1,0:T(2,128)(2,1)S(1)}, bf16[1024,2,128]{2,1,0:T(2,128)(2,1)}, u32[]{:S(2)}) copy-start(bf16[1024,2,128]{2,1,0:T(2,128)(2,1)} %reshape.172) | copy-start | bytes 1572868
  411.7 15.2 %copy-start.13 = (s32[1024]{0:T(1024)S(1)}, s32[1024]{0:T(1024)}, u32[]{:S(2)}) copy-start(s32[1024]{0:T(1024)} %copy-done.12) | copy-start | bytes 12292
  417.5 6.7 copy-start.7
  426.9 0.7 copy-start.11
  631.0 8.3 %copy-start.14 = (pred[7168]{0:T(1024)(128)(4,1)S(1)}, pred[7168]{0:T(1024)(128)(4,1)}, u32[]{:S(2)}) copy-start(pred[7168]{0:T(1024)(128)(4,1)} %broadcast_in_dim.172) | copy-start | bytes 21508
  639.3 71.6 %copy-start.1 = (s32[32,56]{1,0:T(8,128)S(1)}, s32[32,56]{1,0:T(8,128)}, u32[]{:S(2)}) copy-start(s32[32,56]{1,0:T(8,128)} %param.30) | copy-start | bytes 21508
Sparse Core Ops, SparseCore 0:
  16.5 45.2 all-gather.5
  63.4 41.3 all-gather.11
  106.5 24.0 all-gather.7
  132.1 24.3 all-gather.13
  158.0 230.8 all-gather.9
  646.8 61.6 reduce-scatter.1
